TPU v7x, 32 devices: a whole 2x2x4 slice. The times are simulated.
32 devices in a mesh: blk: 32 (over z, y, x, core).
Axes of the slice: x: 2, y: 2, z: 4, core: 2. Of those that a mesh axis runs over, the one named last changes fastest.
Arguments:
- single: bfloat16 [512, 384], P('blk'), may hold values from -6 to 6
- angles: float32 [3, 512], P(None, 'blk'), may hold values from -3.140625 to 3.140625
- trans: float32 [3, 512], P(None, 'blk'), may hold values from -6 to 6
- left_factor: bfloat16 [512, 64], P('blk'), may hold values from -6 to 6
- right_factor: bfloat16 [512, 64], P('blk'), may hold values from -6 to 6
- chain: int32 [512], P('blk'), may hold values from 0 to 7, never falling along the last dimension, each value on 1 to 128 neighbouring positions
- live: int32 [512], P('blk'), may hold values 0 or 1
- w_query: bfloat16 [384, 192], replicated, may hold values from -0.3125 to 0.3125
- w_keyval: bfloat16 [384, 384], replicated, may hold values from -0.3125 to 0.3125
- w_qpoints: bfloat16 [384, 144], replicated, may hold values from -0.3125 to 0.3125
- w_kvpoints: bfloat16 [384, 432], replicated, may hold values from -0.3125 to 0.3125
- w_pair_in: bfloat16 [64, 128], replicated, may hold values from -0.75 to 0.75
- chain_bias: float32 [128], replicated, may hold values from -6 to 6
- w_pair_out: bfloat16 [128, 128], replicated, may hold values from -0.5 to 0.5
- w_bias: bfloat16 [128, 12], replicated, may hold values from -0.5 to 0.5
- point_weight: float32 [12], replicated, may hold values from 0.1 to 1
- w_out: bfloat16 [2112, 384], replicated, may hold values from -0.125 to 0.125
- out_gain: float32 [384], replicated, may hold values from 0.5 to 1.5
- w_frame: float32 [384, 6], replicated, may hold values from -0.3125 to 0.3125
Outputs:
- single_out: bfloat16 [512, 384], P('blk')
- frames_out: float32 [12, 512], P(None, 'blk')
Inputs may be any that keep to these rules, and one draw needn't show every extreme that they name: Residues of one chain are consecutive and chain numbers never fall along the residues; a chain has 1 to 128 residues.
All inputs are finite; a program needn't handle non-finite values. No bound on the sum of `live` on one device may be relied on, other than what follows from the above.
Results may differ from a plain program's by a relative error of at most 0.0035.
Values may be sent and summed in bfloat16 or wider, within the bound.
A program may use at most 192 MiB of HBM per device.

v0:
```python
import jax
import jax.numpy as jnp
from jax import lax
from jax.sharding import PartitionSpec as P


def rotation(angles):
    ca, sa = (jnp.cos(angles[0]), jnp.sin(angles[0]))
    cb, sb = (jnp.cos(angles[1]), jnp.sin(angles[1]))
    cc, sc = (jnp.cos(angles[2]), jnp.sin(angles[2]))
    first = jnp.stack([ca * cb, -sa * cc + ca * sb * sc, sa * sc + ca * sb * cc])
    second = jnp.stack([sa * cb, ca * cc + sa * sb * sc, -ca * sc + sa * sb * cc])
    third = jnp.stack([-sb, cb * sc, cb * cc])
    return jnp.stack([first, second, third])


def quat_rotation(bpart, cpart, dpart):
    norm = jnp.sqrt(1.0 + bpart * bpart + cpart * cpart + dpart * dpart)
    apart = 1.0 / norm
    bpart, cpart, dpart = (bpart / norm, cpart / norm, dpart / norm)
    first = jnp.stack(
        [
            apart * apart + bpart * bpart - cpart * cpart - dpart * dpart,
            2.0 * (bpart * cpart - apart * dpart),
            2.0 * (bpart * dpart + apart * cpart),
        ]
    )
    second = jnp.stack(
        [
            2.0 * (bpart * cpart + apart * dpart),
            apart * apart - bpart * bpart + cpart * cpart - dpart * dpart,
            2.0 * (cpart * dpart - apart * bpart),
        ]
    )
    third = jnp.stack(
        [
            2.0 * (bpart * dpart - apart * cpart),
            2.0 * (cpart * dpart + apart * bpart),
            apart * apart - bpart * bpart - cpart * cpart + dpart * dpart,
        ]
    )
    return jnp.stack([first, second, third])


def to_global(rot, shift, points):
    return (
        jnp.einsum("xyn,nyhp->nxhp", rot, points, precision=lax.Precision.HIGHEST)
        + shift.T[:, :, None, None]
    )


def key_side(rows, angles, trans, w_keyval, w_kvpoints, heads):
    count = rows.shape[0]
    keyval = jnp.dot(rows, w_keyval, preferred_element_type=jnp.float32).astype(jnp.bfloat16)
    kvpoints = jnp.dot(rows, w_kvpoints, preferred_element_type=jnp.float32).reshape(
        count, 3, heads, -1
    )
    kvglobal = to_global(rotation(angles), trans, kvpoints).astype(jnp.bfloat16)
    return jnp.concatenate([keyval, kvglobal.reshape(count, -1)], axis=1)


def per_device(
    single,
    angles,
    trans,
    left_factor,
    right_factor,
    chain,
    live,
    w_query,
    w_keyval,
    w_qpoints,
    w_kvpoints,
    w_pair_in,
    chain_bias,
    w_pair_out,
    w_bias,
    point_weight,
    w_out,
    out_gain,
    w_frame,
):
    rows = single.shape[0]
    heads = point_weight.shape[0]
    head_dim = w_query.shape[1] // heads
    qpts = w_qpoints.shape[1] // (3 * heads)
    vpts = w_kvpoints.shape[1] // (3 * heads) - qpts
    pair_dim = w_pair_out.shape[0]
    width = heads * head_dim
    rot = rotation(angles)
    query = (
        jnp.dot(single, w_query, preferred_element_type=jnp.float32)
        .astype(jnp.bfloat16)
        .reshape(rows, heads, head_dim)
    )
    qpoints = jnp.dot(single, w_qpoints, preferred_element_type=jnp.float32).reshape(
        rows, 3, heads, qpts
    )
    qglobal = to_global(rot, trans, qpoints)
    qsq = jnp.sum(qglobal * qglobal, axis=(1, 3)).T
    coef = point_weight * (2.0 / (9.0 * qpts)) ** 0.5 / 2.0
    left_wide = left_factor.astype(jnp.float32)

    def attend(carry, keys):
        packed, right, chain_keys, live_keys = keys
        count = packed.shape[0]
        key_vecs = packed[:, :width].reshape(count, heads, head_dim)
        val_vecs = packed[:, width : 2 * width].reshape(count, heads, head_dim)
        points = packed[:, 2 * width :].reshape(count, 3, heads, qpts + vpts)
        kglobal = points[..., :qpts].astype(jnp.float32)
        vglobal = points[..., qpts:]
        ksq = jnp.sum(kglobal * kglobal, axis=(1, 3)).T
        same = (chain[:, None] == chain_keys[None, :]).astype(jnp.float32)
        prod = (left_wide[:, None, :] * right.astype(jnp.float32)[None, :, :]).astype(jnp.bfloat16)
        hidden = (
            jnp.einsum("qkr,rz->qkz", prod, w_pair_in, preferred_element_type=jnp.float32)
            + same[:, :, None] * chain_bias
        )
        hidden = jax.nn.gelu(hidden, approximate=True).astype(jnp.bfloat16)
        outer = jnp.einsum("qkz,zy->qky", hidden, w_pair_out, preferred_element_type=jnp.float32)
        center = outer - jnp.mean(outer, axis=2, keepdims=True)
        pair = (
            center * lax.rsqrt(jnp.mean(center * center, axis=2, keepdims=True) + 1e-05)
        ).astype(jnp.bfloat16)
        scalar = jnp.einsum(
            "qhc,khc->hqk", query, key_vecs, preferred_element_type=jnp.float32
        ) * head_dim ** (-0.5)
        bias = jnp.einsum("qkz,zh->hqk", pair, w_bias, preferred_element_type=jnp.float32)
        cross = jnp.einsum("qxhp,kxhp->hqk", qglobal, kglobal, precision=lax.Precision.HIGHEST)
        dist = qsq[:, :, None] + ksq[:, None, :] - 2.0 * cross
        dead = 100000.0 * (1.0 - live_keys.astype(jnp.float32))
        logits = (1.0 / 3.0) ** 0.5 * (scalar + bias - coef[:, None, None] * dist) - dead[
            None, None, :
        ]
        top, total, acc_values, acc_points, acc_pair = carry
        new_top = jnp.maximum(top, jnp.max(logits, axis=2))
        factor = jnp.exp(top - new_top)
        terms = jnp.exp(logits - new_top[:, :, None])
        total = total * factor + jnp.sum(terms, axis=2)
        weights = terms.astype(jnp.bfloat16)
        acc_values = acc_values * factor[:, :, None] + jnp.einsum(
            "hqk,khc->hqc", weights, val_vecs, preferred_element_type=jnp.float32
        )
        acc_points = acc_points * factor[:, :, None, None] + jnp.einsum(
            "hqk,kxhp->hqxp", weights, vglobal, preferred_element_type=jnp.float32
        )
        acc_pair = acc_pair * factor[:, :, None] + jnp.einsum(
            "hqk,qkz->hqz", weights, pair, preferred_element_type=jnp.float32
        )
        return (new_top, total, acc_values, acc_points, acc_pair)

    def run_blocks(carry, keys):
        count = keys[0].shape[0]
        if count > 512 and count % 512 == 0:
            stacked = jax.tree.map(
                lambda item: item.reshape((count // 512, 512) + item.shape[1:]), keys
            )
            return lax.scan(lambda state, block: (attend(state, block), None), carry, stacked)[0]
        return attend(carry, keys)

    init = (
        jnp.full((heads, rows), -1e30, jnp.float32),
        jnp.zeros((heads, rows), jnp.float32),
        jnp.zeros((heads, rows, head_dim), jnp.float32),
        jnp.zeros((heads, rows, 3, vpts), jnp.float32),
        jnp.zeros((heads, rows, pair_dim), jnp.float32),
    )
    packed = key_side(single, angles, trans, w_keyval, w_kvpoints, heads)
    state = run_blocks(
        init,
        (
            lax.all_gather(packed, "blk", axis=0, tiled=True),
            lax.all_gather(right_factor, "blk", axis=0, tiled=True),
            lax.all_gather(chain, "blk", axis=0, tiled=True),
            lax.all_gather(live, "blk", axis=0, tiled=True),
        ),
    )
    top, total, acc_values, acc_points, acc_pair = state
    att_values = acc_values / total[:, :, None]
    att_points = acc_points / total[:, :, None, None]
    att_pair = acc_pair / total[:, :, None]
    local = jnp.einsum(
        "yxq,hqyp->hqxp",
        rot,
        att_points - trans.T[None, :, :, None],
        precision=lax.Precision.HIGHEST,
    )
    pnorm = jnp.sqrt(jnp.sum(local * local, axis=2) + 1e-08)
    features = jnp.concatenate(
        [
            att_values.transpose(1, 0, 2).reshape(rows, -1),
            local.transpose(1, 2, 0, 3).reshape(rows, -1),
            pnorm.transpose(1, 0, 2).reshape(rows, -1),
            att_pair.transpose(1, 0, 2).reshape(rows, -1),
        ],
        axis=1,
    ).astype(jnp.bfloat16)
    mixed = jnp.dot(features, w_out, preferred_element_type=jnp.float32) + single.astype(
        jnp.float32
    )
    center = mixed - jnp.mean(mixed, axis=1, keepdims=True)
    snew = center * lax.rsqrt(jnp.mean(center * center, axis=1, keepdims=True) + 1e-05) * out_gain
    update = jnp.dot(snew, w_frame, precision=lax.Precision.HIGHEST)
    upd_rot = quat_rotation(update[:, 0], update[:, 1], update[:, 2])
    new_rot = jnp.einsum("xyn,yzn->xzn", rot, upd_rot, precision=lax.Precision.HIGHEST)
    new_trans = (
        jnp.einsum("xyn,yn->xn", rot, update[:, 3:].T, precision=lax.Precision.HIGHEST) + trans
    )
    frames_out = jnp.concatenate([new_rot.reshape(9, rows), new_trans], axis=0)
    return (snew.astype(jnp.bfloat16), frames_out)


def solution(mesh):
    in_specs = (
        P("blk", None),
        P(None, "blk"),
        P(None, "blk"),
        P("blk", None),
        P("blk", None),
        P("blk"),
        P("blk"),
        P(),
        P(),
        P(),
        P(),
        P(),
        P(),
        P(),
        P(),
        P(),
        P(),
        P(),
        P(),
    )
    out_specs = (P("blk", None), P(None, "blk"))
    return jax.shard_map(
        per_device, mesh=mesh, in_specs=in_specs, out_specs=out_specs, check_vma=False
    )
```

profile of v0, /device:TPU:1, one launch (start us, length us, event | category | flops | bytes accessed | tf_op | source)
XLA Modules:
  0.0 156.8 jit_solution(12489335945041852786)
XLA Ops:
  0.7 0.8 broadcast_multiply_fusion.2
  1.4 0.8 multiply_add_fusion
  2.3 0.9 dynamic-update-slice
  3.1 0.8 dynamic-update-slice.1
  4.0 40.5 %all-reduce.2 = (s32[512]{0:T(512)S(1)}, s32[512]{0:T(512)S(1)}) all-reduce(s32[512]{0:T(512)S(1)} %dynamic-update-slice, s32[512]{0:T(512)S(1)} %dynamic-update-slice.1), channel_id=1, replica_groups=mesh['blk'=32] {'blk'}, use_global_device_ids=true, to_apply=%add | all-reduce | flops 1024 | bytes 8192
  44.5 0.8 fusion.58
  45.4 0.8 copy.151
  46.1 0.7 convert_element_type.50
  46.8 1.1 convolution_convert_fusion.1
  47.9 1.1 convolution_convert_fusion
  49.1 0.7 copy.181
  49.8 0.7 compare_convert_fusion
  50.6 1.2 fusion.69
  51.9 1.1 fusion.70
  53.9 42.2 %all_gather.13 = bf16[512,64]{1,0:T(8,128)(2,1)S(1)} all-gather(bf16[16,64]{1,0:T(8,128)(2,1)} %param.23), channel_id=1, replica_groups=mesh['blk'=32] {'blk'}, dimensions={0}, use_global_device_ids=true | all-gather | bytes 67584 | tf_op jit(solution)/shard_map/all_gather | solution.py:173
  96.4 1.0 fusion.16
  97.6 39.3 %all_gather.12 = bf16[512,816]{1,0:T(8,128)(2,1)S(1)} all-gather(bf16[16,816]{1,0:T(8,128)(2,1)S(1)} %pad_maximum_fusion), channel_id=1, replica_groups=mesh['blk'=32] {'blk'}, dimensions={0}, use_global_device_ids=true | all-gather | bytes 861696 | tf_op jit(solution)/shard_map/all_gather | solution.py:172
  137.9 5.4 %fusion.64 = (f32[16,512]{1,0:T(8,128)S(1)}, f32[16,512,128]{1,2,0:T(8,128)}) fusion(bf16[128,128]{1,0:T(8,128)(2,1)S(1)} %copy-done.7, f32[128]{0:T(128)S(1)} %copy-done.9, f32[16,512]{1,0:T(8,128)S(1)} %compare_convert_fusion, f32[512,64]{0,1:T(8,128)S(1)} %convert_element_type.51, f32[16,64]{1,0:T(8,128)S(1)} %convert_element_type.50, ...), kind=kOutput, calls=%fused_computation.134 | convolution fusion | flops 416276480 | bytes 4444672 | tf_op jit(solution)/shard_map/qkz,zy->qky/dot_general | solution.py:120
  143.3 3.0 %multiply_reduce_fusion = f32[16,512]{1,0:T(8,128)S(1)} fusion(f32[16,512,128]{1,2,0:T(8,128)} %get-tuple-element.37, f32[16,512]{1,0:T(8,128)S(1)} %broadcast_multiply_fusion), kind=kLoop, calls=%fused_computation.10 | loop fusion | flops 3137536 | bytes 4259840 | tf_op jit(solution)/shard_map/reduce_sum | solution.py:123
  146.7 0.7 fusion.28
  149.1 2.8 %fusion.20 = bf16[16,12,128]{2,1,0:T(8,128)(2,1)S(1)} fusion(f32[16,512,128]{1,2,0:T(8,128)} %get-tuple-element.37, f32[16,512]{1,0:T(8,128)S(1)} %add_rsqrt_fusion, f32[16,512]{1,0:T(8,128)S(1)} %broadcast_multiply_fusion, bf16[12,16,512]{2,1,0:T(8,128)(2,1)S(1)} %get-tuple-element.12, f32[16,12]{1,0:T(8,128)S(1)} %copy.177, f32[16,12]{1,0:T(8,128)S(1)} %copy.174), kind=kOutput, calls=%fused_computation.30 | convolution fusion | flops 28385280 | bytes 4507136 | tf_op jit(solution)/shard_map/hqk,qkz->hqz/dot_general | solution.py:147
  152.5 0.7 multiply_reduce_fusion.2
  154.9 0.7 fusion.40
  156.2 0.6 pad_maximum_fusion.1
  (85 shorter events, 7.3 us)
Async XLA Ops:
  0.6 153.4 %copy-start = (bf16[2112,384]{1,0:T(8,128)(2,1)S(1)}, bf16[2112,384]{1,0:T(8,128)(2,1)}, u32[]{:S(2)}) copy-start(bf16[2112,384]{1,0:T(8,128)(2,1)} %param.35) | copy-start | bytes 4866052
  53.9 84.0 %copy-start.7 = (bf16[128,128]{1,0:T(8,128)(2,1)S(1)}, bf16[128,128]{1,0:T(8,128)(2,1)}, u32[]{:S(2)}) copy-start(bf16[128,128]{1,0:T(8,128)(2,1)} %param.32) | copy-start | bytes 98308
  53.9 84.0 %copy-start.9 = (f32[128]{0:T(128)S(1)}, f32[128]{0:T(128)}, u32[]{:S(2)}) copy-start(f32[128]{0:T(128)} %param.31) | copy-start | bytes 1540
  143.3 3.4 %copy-start.1 = (f32[16,512,128]{1,2,0:T(8,128)S(1)}, f32[16,512,128]{1,2,0:T(8,128)}, u32[]{:S(2)}) copy-start(f32[16,512,128]{1,2,0:T(8,128)} %get-tuple-element.37) | copy-start | bytes 12582916
  143.3 3.4 %copy-start.5 = (bf16[128,12]{0,1:T(8,128)(2,1)S(1)}, bf16[128,12]{0,1:T(8,128)(2,1)}, u32[]{:S(2)}) copy-start(bf16[128,12]{0,1:T(8,128)(2,1)} %param.33) | copy-start | bytes 9220
  146.7 2.1 %copy-start.4 = (f32[3,16]{1,0:T(4,128)S(1)}, f32[3,16]{1,0:T(4,128)}, u32[]{:S(2)}) copy-start(f32[3,16]{1,0:T(4,128)} %param.21) | copy-start | bytes 580
  148.8 5.2 %copy-start.2 = (bf16[16,384]{1,0:T(8,128)(2,1)S(1)}, bf16[16,384]{1,0:T(8,128)(2,1)}, u32[]{:S(2)}) copy-start(bf16[16,384]{1,0:T(8,128)(2,1)} %param.19) | copy-start | bytes 36868
  149.0 5.6 %copy-start.6 = (f32[384]{0:T(512)S(1)}, f32[384]{0:T(512)}, u32[]{:S(2)}) copy-start(f32[384]{0:T(512)} %param.36) | copy-start | bytes 4612
  149.1 5.6 %copy-start.8 = (f32[384,6]{0,1:T(8,128)S(1)}, f32[384,6]{0,1:T(8,128)}, u32[]{:S(2)}) copy-start(f32[384,6]{0,1:T(8,128)} %param.37) | copy-start | bytes 27652
  149.1 6.7 %copy-start.3 = (f32[3,3,16]{1,0,2:T(4,128)S(1)}, f32[3,3,16]{1,0,2:T(4,128)}, u32[]{:S(2)}) copy-start(f32[3,3,16]{1,0,2:T(4,128)} %copy.181) | copy-start | bytes 1732
where the time goes:
time: 158 us; the launch traced here: 157 us
  blocking collectives  122 us (77%)
  matrix products  17.7 us (11%)
  other arithmetic  8.91 us (6%)
  local copies, waits for them, and re-layouts  7.06 us (4%)
    all_gather x1, blocking collectives, per_device(): lax.all_gather(right_factor, 'blk', axis=0, tiled=True)  42.2 us
    unnamed x1, blocking collectives  40.5 us
    all_gather x1, blocking collectives, per_device(): lax.all_gather(packed, 'blk', axis=0, tiled=True)  39.3 us
    dot_general x1, matrix products, attend(): jnp.einsum('qkz,zy->qky', hidden, w_pair_out, preferred_element_type=jnp....  5.39 us

commit v1 on v0

v1 whole, which is shorter than its diff:
```python
import functools

import jax
import jax.numpy as jnp
from jax import lax
from jax.experimental import pallas as pl
from jax.experimental.pallas import tpu as pltpu
from jax.sharding import PartitionSpec as P

F32 = jnp.float32
BF16 = jnp.bfloat16
MESH = pl.DeviceIdType.MESH
HP = 16
CHAINS = 8
AUX = 128


def rotation(angles):
    ca, sa = (jnp.cos(angles[0]), jnp.sin(angles[0]))
    cb, sb = (jnp.cos(angles[1]), jnp.sin(angles[1]))
    cc, sc = (jnp.cos(angles[2]), jnp.sin(angles[2]))
    return [
        ca * cb, -sa * cc + ca * sb * sc, sa * sc + ca * sb * cc,
        sa * cb, ca * cc + sa * sb * sc, -ca * sc + sa * sb * cc,
        -sb, cb * sc, cb * cc,
    ]


def dot(a, b):
    return jnp.dot(a, b, preferred_element_type=F32)


def dot_t(a, b):
    return lax.dot_general(a, b, (((1,), (1,)), ((), ())), preferred_element_type=F32)


def split3(x):
    hi = x.astype(BF16)
    rest = x - hi.astype(F32)
    mid = rest.astype(BF16)
    lo = (rest - mid.astype(F32)).astype(BF16)
    return hi, mid, lo


def onehot(mask):
    return jnp.where(mask, 1.0, 0.0).astype(BF16)


def iota(shape, dim):
    return lax.broadcasted_iota(jnp.int32, shape, dim)


def frame_columns(aux, base):
    wide = aux.astype(F32)
    return (
        wide[:, base : base + 12] + wide[:, base + 12 : base + 24] + wide[:, base + 24 : base + 36]
    )


def kernel(
    n, dims, payload, left, coef_in, w_pair_in, chain_bias, w_pair_out, w_bias, out_gain, w_frame,
    w_query_h, w_keyval_h, w_qpoints_h, w_kvpoints_h, w_out_h,
    single_out, frames_out,
    gat, w_query, w_keyval, w_qpoints, w_kvpoints, w_out, kv, kg, logit, wts, pair, attp, scale,
    win2, wout2, dead,
    send_sem, recv_sem, relay_sem, own_sem, w_sem,
):
    heads, head_dim, qpts, vpts, rank, pair_dim = dims
    rows, cs = single_out.shape
    keys = n * rows
    width = heads * head_dim
    pts = qpts + vpts
    pw = heads * pts
    fbase = rank + 3 * CHAINS
    third = (1.0 / 3.0) ** 0.5
    me = lax.axis_index("blk")
    chips = n // 2
    core = me % 2
    chip = me // 2
    sib = chip * 2 + 1 - core

    loads = [
        pltpu.make_async_copy(src, dst, w_sem.at[i])
        for i, (src, dst) in enumerate(
            [
                (w_query_h, w_query),
                (w_qpoints_h, w_qpoints),
                (w_keyval_h, w_keyval),
                (w_kvpoints_h, w_kvpoints),
                (w_out_h, w_out),
            ]
        )
    ]
    barrier = pltpu.get_barrier_semaphore()

    def peer_of(d):
        return ((chip + d) % chips) * 2 + core

    def block(dev):
        return gat.at[pl.ds(pl.multiple_of(dev * rows, rows), rows), :]

    @pl.loop(1, chips)
    def _(d):
        pl.semaphore_signal(barrier, inc=1, device_id=(peer_of(d),), device_id_type=MESH)

    pl.semaphore_signal(barrier, inc=1, device_id=(sib,), device_id_type=MESH)
    own = pltpu.make_async_copy(payload, block(me), own_sem)
    own.start()
    for item in loads:
        item.start()
    pl.semaphore_wait(barrier, chips)

    def send(dev):
        return pltpu.make_async_remote_copy(
            src_ref=payload, dst_ref=block(me), send_sem=send_sem.at[dev], recv_sem=recv_sem.at[me],
            device_id=(dev,), device_id_type=MESH,
        )

    def arrival(dev):
        return pltpu.make_async_remote_copy(
            src_ref=payload, dst_ref=block(dev), send_sem=send_sem.at[dev],
            recv_sem=recv_sem.at[dev], device_id=(sib,), device_id_type=MESH,
        )

    def relay(dev):
        return pltpu.make_async_remote_copy(
            src_ref=block(dev), dst_ref=block(dev), send_sem=relay_sem.at[dev],
            recv_sem=recv_sem.at[dev], device_id=(sib,), device_id_type=MESH,
        )

    @pl.loop(1, chips)
    def _(d):
        send(peer_of(d)).start()

    send(sib).start()

    own_x = payload[:, :cs]
    own_frame = frame_columns(payload[:, cs:], fbase)
    loads[0].wait()
    loads[1].wait()
    query = dot(own_x, w_query[...]).astype(BF16).astype(F32)
    hrow = iota((rows, HP, width), 1)
    lane = iota((rows, HP, width), 2)
    vmask = ((lane >= hrow * head_dim) & (lane < (hrow + 1) * head_dim)).reshape(rows * HP, width)
    a_query = jnp.where(
        vmask, jnp.broadcast_to(query[:, None, :], (rows, HP, width)).reshape(rows * HP, width), 0.0
    ).astype(BF16)
    part = heads * qpts
    spread = jnp.where(
        (iota((part, pw), 0) // qpts) * pts + iota((part, pw), 0) % qpts == iota((part, pw), 1), 1.0, 0.0
    ).astype(BF16)
    qp = [
        dot(own_x, dot(w_qpoints[:, y * part : (y + 1) * part], spread).astype(BF16))
        for y in range(3)
    ]
    hrow = iota((rows, HP, pw), 1)
    lane = iota((rows, HP, pw), 2)
    kmask = ((lane >= hrow * pts) & (lane < hrow * pts + qpts)).reshape(rows * HP, pw)
    amask = ((lane >= hrow * pts) & (lane < (hrow + 1) * pts)).reshape(rows * HP, pw)
    a_points = []
    qsum = 0.0
    for x in range(3):
        point = own_frame[:, 9 + x : 10 + x]
        for y in range(3):
            point = point + own_frame[:, 3 * x + y : 3 * x + y + 1] * qp[y]
        a_x = jnp.where(
            kmask, jnp.broadcast_to(point[:, None, :], (rows, HP, pw)).reshape(rows * HP, pw), 0.0
        )
        qsum = qsum + a_x * a_x
        a_points.append(split3(a_x))
    qsq = jnp.sum(qsum, axis=1, keepdims=True)
    coef16 = coef_in[...]
    coef = jnp.broadcast_to(coef16[None], (rows, HP, 1)).reshape(rows * HP, 1)

    bias_parts = [
        jnp.broadcast_to(item.astype(F32), (CHAINS, pair_dim)) for item in split3(chain_bias[...])
    ]
    w_in = jnp.concatenate(
        [w_pair_in[...].astype(F32)] + bias_parts + [jnp.zeros((AUX - fbase, pair_dim), F32)], axis=0
    ).astype(BF16)
    none = jnp.zeros((pair_dim, pair_dim), BF16)
    win2[...] = jnp.concatenate(
        [jnp.concatenate([w_in, none], axis=1), jnp.concatenate([none, w_in], axis=1)], axis=0
    )
    w_o = w_pair_out[...]
    wout2[...] = jnp.concatenate(
        [jnp.concatenate([w_o, none], axis=1), jnp.concatenate([none, w_o], axis=1)], axis=0
    )
    eye = onehot(iota((HP, heads), 0) == iota((HP, heads), 1))
    w_b = dot_t(eye, w_bias[...]).astype(BF16)
    none = jnp.zeros((HP, pair_dim), BF16)
    w_b2 = jnp.concatenate(
        [jnp.concatenate([w_b, none], axis=1), jnp.concatenate([none, w_b], axis=1)], axis=0
    )

    @pl.loop(1, chips)
    def _(d):
        dev = peer_of(d)
        arrival(dev).wait_recv()
        relay(dev).start()

    own.wait()
    loads[2].wait()
    loads[3].wait()
    arrival(sib).wait_recv()

    @pl.loop(1, chips)
    def _(d):
        arrival(((chip + d) % chips) * 2 + 1 - core).wait_recv()

    kb = 128
    hrow = iota((HP, pw), 0)
    lane = iota((HP, pw), 1)
    hsel = onehot((lane >= hrow * pts) & (lane < hrow * pts + qpts))
    live_sel = onehot(iota((HP, AUX), 1) == fbase + 36)

    @pl.loop(0, keys // kb)
    def _(b):
        at = pl.ds(pl.multiple_of(b * kb, kb), kb)
        x_in = gat[at, :cs]
        aux = gat[at, cs:]
        keyval = dot(x_in, w_keyval[...]).astype(BF16)
        kv[at, :] = keyval
        kp = dot(x_in, w_kvpoints[...])
        frame = frame_columns(aux, fbase)
        scalar = dot_t(a_query, keyval[:, :width]) * head_dim ** (-0.5)
        cross = 0.0
        square = 0.0
        for x in range(3):
            point = frame[:, 9 + x : 10 + x]
            for y in range(3):
                point = point + frame[:, 3 * x + y : 3 * x + y + 1] * kp[:, y * pw : (y + 1) * pw]
            point = point.astype(BF16)
            kg[x, at, :] = point
            wide = point.astype(F32)
            square = square + wide * wide
            for item in a_points[x]:
                cross = cross + dot_t(item, point)
        ksq = 0.0
        for item in split3(square):
            ksq = ksq + dot_t(hsel, item)
        ksq = jnp.broadcast_to(ksq[None], (rows, HP, kb)).reshape(rows * HP, kb)
        logit[:, at] = scalar - coef * (qsq + ksq - 2.0 * cross)
        dead[:, at] = 100000.0 * (1.0 - dot_t(live_sel, aux))

    @pl.loop(0, rows // 2)
    def _(t):
        left0 = left[pl.ds(2 * t, 1), :]
        left1 = left[pl.ds(2 * t + 1, 1), :]

        @pl.loop(0, keys // kb, unroll=2)
        def _(b):
            at = pl.ds(pl.multiple_of(b * kb, kb), kb)
            right = gat[at, cs:].astype(F32)
            prod = jnp.concatenate(
                [(right * left0).astype(BF16), (right * left1).astype(BF16)], axis=1
            )
            hidden = dot(prod, win2[...])
            hidden = jax.nn.gelu(hidden, approximate=True).astype(BF16)
            outer = dot(hidden, wout2[...])
            for half in range(2):
                o = outer[:, half * pair_dim : (half + 1) * pair_dim]
                center = o - jnp.mean(o, axis=1, keepdims=True)
                var = jnp.mean(center * center, axis=1, keepdims=True)
                pair[at, half * pair_dim : (half + 1) * pair_dim] = (
                    center * lax.rsqrt(var + 1e-05)
                ).astype(BF16)

        sel = pl.ds(pl.multiple_of(t * 2 * HP, 2 * HP), 2 * HP)
        both = pair[...]
        bias = dot_t(w_b2, both)
        row = third * (logit[sel, :] + bias) - jnp.concatenate([dead[...], dead[...]], axis=0)
        top = jnp.max(row, axis=1, keepdims=True)
        terms = jnp.exp(row - top)
        inv = 1.0 / jnp.sum(terms, axis=1, keepdims=True)
        weight = terms.astype(BF16)
        wts[sel, :] = weight
        scale[sel, :] = jnp.broadcast_to(inv, (2 * HP, 128))
        out = dot(weight, both) * inv
        attp[sel, :] = jnp.concatenate([out[:HP, :pair_dim], out[HP:, pair_dim:]], axis=0)

    weight = wts[...]
    inv = scale[:, :1]

    def pick(value, mask):
        value = jnp.where(mask, value * inv, 0.0)
        return jnp.sum(value.reshape(rows, HP, value.shape[1]), axis=1)

    values = pick(dot(weight, kv[:, width:]), vmask)
    away = [
        pick(dot(weight, kg[y]), amask) - own_frame[:, 9 + y : 10 + y] for y in range(3)
    ]
    out_cols = heads * vpts
    narrow = jnp.where(
        iota((pw, out_cols), 0)
        == (iota((pw, out_cols), 1) // vpts) * pts + qpts + iota((pw, out_cols), 1) % vpts,
        1.0, 0.0,
    ).astype(BF16)
    loads[4].wait()
    mixed = own_x.astype(F32) + dot(values.astype(BF16), w_out[:width, :])
    norm = 0.0
    for x in range(3):
        local = 0.0
        for y in range(3):
            local = local + own_frame[:, 3 * y + x : 3 * y + x + 1] * away[y]
        norm = norm + local * local
        item = dot(local.astype(BF16), narrow).astype(BF16)
        first = width + x * out_cols
        mixed = mixed + dot(item, w_out[first : first + out_cols, :])
    item = dot(jnp.sqrt(norm + 1e-08).astype(BF16), narrow).astype(BF16)
    first = width + 3 * out_cols
    mixed = mixed + dot(item, w_out[first : first + out_cols, :])
    first = first + out_cols
    for h in range(heads):
        item = attp[pl.ds(h, rows, stride=HP), :].astype(BF16)
        mixed = mixed + dot(item, w_out[first + h * pair_dim : first + (h + 1) * pair_dim, :])

    center = mixed - jnp.mean(mixed, axis=1, keepdims=True)
    var = jnp.mean(center * center, axis=1, keepdims=True)
    snew = center * lax.rsqrt(var + 1e-05) * out_gain[...]
    single_out[...] = snew.astype(BF16)
    update = jnp.dot(snew, w_frame[...], precision=lax.Precision.HIGHEST, preferred_element_type=F32)
    table = jnp.concatenate([update, own_frame, jnp.zeros((rows, 110), F32)], axis=1).T
    b, c, d = table[0:1], table[1:2], table[2:3]
    size = jnp.sqrt(1.0 + b * b + c * c + d * d)
    a = 1.0 / size
    b, c, d = b / size, c / size, d / size
    ru = [
        [a * a + b * b - c * c - d * d, 2.0 * (b * c - a * d), 2.0 * (b * d + a * c)],
        [2.0 * (b * c + a * d), a * a - b * b + c * c - d * d, 2.0 * (c * d - a * b)],
        [2.0 * (b * d - a * c), 2.0 * (c * d + a * b), a * a - b * b - c * c + d * d],
    ]
    rot = [[table[6 + 3 * x + y : 7 + 3 * x + y] for y in range(3)] for x in range(3)]
    for x in range(3):
        for z in range(3):
            frames_out[3 * x + z : 3 * x + z + 1, :] = (
                rot[x][0] * ru[0][z] + rot[x][1] * ru[1][z] + rot[x][2] * ru[2][z]
            )
        frames_out[9 + x : 10 + x, :] = (
            rot[x][0] * table[3:4] + rot[x][1] * table[4:5] + rot[x][2] * table[5:6]
            + table[15 + x : 16 + x]
        )

    @pl.loop(1, chips)
    def _(d):
        dev = peer_of(d)
        send(dev).wait_send()
        relay(dev).wait_send()

    send(sib).wait_send()


def exact_split(x):
    hi = lax.reduce_precision(x, 8, 7)
    mid = lax.reduce_precision(x - hi, 8, 7)
    return [hi, mid, x - hi - mid]


def per_device(
    n, single, angles, trans, left_factor, right_factor, chain, live, w_query, w_keyval, w_qpoints,
    w_kvpoints, w_pair_in, chain_bias, w_pair_out, w_bias, point_weight, w_out, out_gain, w_frame,
):
    rows, cs = single.shape
    heads = point_weight.shape[0]
    head_dim = w_query.shape[1] // heads
    qpts = w_qpoints.shape[1] // (3 * heads)
    vpts = w_kvpoints.shape[1] // (3 * heads) - qpts
    rank, pair_dim = w_pair_in.shape
    keys = n * rows
    frame = jnp.stack(rotation(angles) + [trans[0], trans[1], trans[2]]).T
    hot = (chain[:, None] == jnp.arange(CHAINS)[None, :]).astype(BF16)
    pad = AUX - rank - 3 * CHAINS - 37
    payload = jnp.concatenate(
        [single, right_factor, hot, hot, hot]
        + [item.astype(BF16) for item in exact_split(frame)]
        + [live.astype(BF16)[:, None], jnp.zeros((rows, pad), BF16)],
        axis=1,
    )
    left = jnp.concatenate(
        [left_factor, hot, hot, hot, jnp.zeros((rows, pad + 37), BF16)], axis=1
    ).astype(F32)
    coef = jnp.pad(point_weight * (2.0 / (9.0 * qpts)) ** 0.5 / 2.0, (0, HP - heads))[:, None]
    vmem = pl.BlockSpec(memory_space=pltpu.VMEM)
    hbm = pl.BlockSpec(memory_space=pl.ANY)
    pw = heads * (qpts + vpts)
    return pl.pallas_call(
        functools.partial(kernel, n, (heads, head_dim, qpts, vpts, rank, pair_dim)),
        out_shape=(
            jax.ShapeDtypeStruct((rows, cs), BF16),
            jax.ShapeDtypeStruct((12, rows), F32),
        ),
        in_specs=[vmem] * 9 + [hbm] * 5,
        out_specs=(vmem, vmem),
        scratch_shapes=[
            pltpu.VMEM((keys, cs + AUX), BF16),
            pltpu.VMEM(w_query.shape, BF16),
            pltpu.VMEM(w_keyval.shape, BF16),
            pltpu.VMEM(w_qpoints.shape, BF16),
            pltpu.VMEM(w_kvpoints.shape, BF16),
            pltpu.VMEM(w_out.shape, BF16),
            pltpu.VMEM((keys, w_keyval.shape[1]), BF16),
            pltpu.VMEM((3, keys, pw), BF16),
            pltpu.VMEM((rows * HP, keys), F32),
            pltpu.VMEM((rows * HP, keys), BF16),
            pltpu.VMEM((keys, 2 * pair_dim), BF16),
            pltpu.VMEM((rows * HP, pair_dim), F32),
            pltpu.VMEM((rows * HP, 128), F32),
            pltpu.VMEM((2 * AUX, 2 * pair_dim), BF16),
            pltpu.VMEM((2 * pair_dim, 2 * pair_dim), BF16),
            pltpu.VMEM((HP, keys), F32),
            pltpu.SemaphoreType.DMA((n,)),
            pltpu.SemaphoreType.DMA((n,)),
            pltpu.SemaphoreType.DMA((n,)),
            pltpu.SemaphoreType.DMA,
            pltpu.SemaphoreType.DMA((5,)),
        ],
        compiler_params=pltpu.CompilerParams(
            collective_id=0, has_side_effects=True, vmem_limit_bytes=50 * 1024 * 1024
        ),
    )(
        payload, left, coef, w_pair_in, chain_bias[None, :], w_pair_out, w_bias, out_gain[None, :],
        w_frame, w_query, w_keyval, w_qpoints, w_kvpoints, w_out,
    )


def solution(mesh):
    row = P("blk", None)
    col = P(None, "blk")
    in_specs = (row, col, col, row, row, P("blk"), P("blk")) + (P(),) * 12
    return jax.shard_map(
        functools.partial(per_device, mesh.shape["blk"]),
        mesh=mesh, in_specs=in_specs, out_specs=(row, col), check_vma=False,
    )
```

time: 158 us -> 45.9 us (0.29)
  blocking collectives: 122 us -> 0 us
  Pallas kernels: 0 us -> 31.5 us
  matrix products: 17.7 us -> 0 us
  other arithmetic: 8.91 us -> 2.2 us
  local copies, waits for them, and re-layouts: 7.06 us -> 10.6 us
    all_gather x2 -> x0, blocking collectives: 81.6 us -> none  [the longest x1 42.2 us: per_device(): lax.all_gather(right_factor, 'blk', axis=0, tiled=True)]
    unnamed x1 -> x0, blocking collectives: 40.5 us -> none
    pallas_call x0 -> x1, Pallas kernels: none -> 31.5 us  [per_device(): pl.pallas_call(functools.partial(kernel, n, (heads, head_dim, qpts, vpts,...]
    dot_general x17 -> x0, matrix products: 17.7 us -> none  [the longest x1 5.39 us: attend(): jnp.einsum('qkz,zy->qky', hidden, w_pair_out, preferred_element_type=jnp....]
    unnamed x25 -> x21, local copies, waits for them, and re-layouts: 2.23 us -> 7.11 us
    reduce_sum x4 -> x0, other arithmetic: 3.47 us -> none  [the longest x1 2.96 us: attend(): jnp.mean(center * center, axis=2, keepdims=True) + 1e-05]
where the time goes in v1:
time: 45.9 us; the launch traced here: 45 us
  Pallas kernels  31.5 us (69%)
  local copies, waits for them, and re-layouts  10.6 us (23%)
  other arithmetic  2.2 us (5%)
  between operations  0.78 us (2%)
    pallas_call x1, Pallas kernels, per_device(): pl.pallas_call(functools.partial(kernel, n, (heads, head_dim, qpts, vpts,...  31.5 us
    unnamed x21, local copies, waits for them, and re-layouts  7.11 us

profile of v1, /device:TPU:1, one launch (start us, length us, event | category | flops | bytes accessed | tf_op | source)
XLA Modules:
  0.0 45.0 jit_solution(14168492905633231597)
XLA Ops:
  0.6 0.0 copy-start
  0.7 0.8 %convert_bitcast_fusion = bf16[16,1]{0,1:T(2,128)(2,1)S(1)} fusion(s32[16]{0:T(128)} %param.25), kind=kLoop, calls=%fused_computation.12 | loop fusion | flops 16 | bytes 96 | tf_op jit(solution)/shard_map/broadcast_in_dim | solution.py:376
  1.5 0.7 %broadcast_multiply_fusion = f32[12]{0:T(128)S(1)} fusion(f32[12]{0:T(128)} %param.34), kind=kLoop, calls=%fused_computation.13 | loop fusion | flops 12 | bytes 96 | tf_op jit(solution)/shard_map/div | solution.py:382
  2.1 0.7 %broadcast_in_dim.25.out_gain = f32[1,384]{1,0:T(1,128)S(1)} reshape(f32[384]{0:T(512)} %param.36) | data formatting | bytes 3072 | tf_op jit(solution)/shard_map/broadcast_in_dim | solution.py:421
  2.8 0.8 %fusion.5 = (f32[1,16]{1,0:T(1,128)S(1)}, f32[1,16]{1,0:T(1,128)S(1)}, f32[1,16]{1,0:T(1,128)S(1)}) fusion(f32[3,16]{1,0:T(4,128)} %param.20), kind=kLoop, calls=%fused_computation.17 | loop fusion | bytes 384 | tf_op jit(solution)/shard_map/slice | solution.py:21
  3.6 0.1 copy.36
  3.7 0.7 %fusion.1 = bf16[16,8]{1,0:T(8,128)(2,1)S(1)} fusion(s32[16]{0:T(128)} %param.24), kind=kLoop, calls=%fused_computation.10 | loop fusion | flops 256 | bytes 320 | tf_op jit(solution)/shard_map/convert_element_type | solution.py:371
  4.4 0.8 %concatenate.7 = bf16[16,128]{1,0:T(8,128)(2,1)S(1)} concatenate(bf16[16,64]{1,0:T(8,128)(2,1)} %param.22, bf16[16,8]{1,0:T(8,128)(2,1)S(1)} %fusion.1, bf16[16,8]{1,0:T(8,128)(2,1)S(1)} %fusion.1, bf16[16,8]{1,0:T(8,128)(2,1)S(1)} %fusion.1, bf16[16,40]{1,0:T(8,128)(2,1)S(1)} %broadcast_in_dim.22), dimensions={1} | concatenate | bytes 8192 | tf_op jit(solution)/shard_map/concatenate | solution.py:379
  5.2 0.1 copy.45
  5.3 0.1 copy.37.coef_in
  5.4 0.1 copy.44
  5.5 0.1 copy.43
  5.6 0.8 %copy.35 = f32[3,16]{0,1:T(8,128)S(1)} copy(f32[3,16]{1,0:T(4,128)} %param.21) | data formatting | bytes 384 | tf_op args[2]
  6.4 0.1 fusion.2
  6.5 0.1 stack.3
  6.6 0.8 %concatenate.6.payload = bf16[16,512]{1,0:T(8,128)(2,1)S(1)} concatenate(bf16[16,384]{1,0:T(8,128)(2,1)} %param.19, bf16[16,64]{1,0:T(8,128)(2,1)} %param.23, bf16[16,8]{1,0:T(8,128)(2,1)S(1)} %fusion.1, bf16[16,8]{1,0:T(8,128)(2,1)S(1)} %fusion.1, bf16[16,8]{1,0:T(8,128)(2,1)S(1)} %fusion.1, bf16[16,12]{1,0:T(8,128)(2,1)S(1)} %get-tuple-element.8, ...), dimensions={1} | concatenate | bytes 32768 | tf_op jit(solution)/shard_map/concatenate | solution.py:373
  7.4 0.8 %copy.38.w_bias = bf16[128,12]{1,0:T(8,128)(2,1)S(1)} copy(bf16[128,12]{0,1:T(8,128)(2,1)} %param.33) | data formatting | bytes 6144 | tf_op args[14]
  8.2 1.0 %copy.40.w_query_h = bf16[384,192]{1,0:T(8,128)(2,1)S(1)} copy(bf16[384,192]{0,1:T(8,128)(2,1)} %param.26) | data formatting | bytes 294912 | tf_op args[7]
  9.3 1.0 %copy.41.w_qpoints_h = bf16[384,144]{1,0:T(8,128)(2,1)S(1)} copy(bf16[384,144]{0,1:T(8,128)(2,1)} %param.28) | data formatting | bytes 221184 | tf_op args[9]
  10.3 0.8 %copy.39.w_frame = f32[384,6]{1,0:T(8,128)S(1)} copy(f32[384,6]{0,1:T(8,128)} %param.37) | data formatting | bytes 18432 | tf_op args[18]
  11.1 1.1 %copy.42.w_kvpoints_h = bf16[384,432]{1,0:T(8,128)(2,1)S(1)} copy(bf16[384,432]{0,1:T(8,128)(2,1)} %param.29) | data formatting | bytes 663552 | tf_op args[10]
  12.3 31.5 %shard_map.194 = (bf16[16,384]{1,0:T(8,128)(2,1)S(1)}, f32[12,16]{1,0:T(8,128)S(1)}) custom-call(bf16[16,512]{1,0:T(8,128)(2,1)S(1)} %concatenate.6.payload, f32[16,128]{1,0:T(8,128)S(1)} %convert_element_type.25.left, f32[16,1]{1,0:T(8,128)S(1)} %copy.37.coef_in, bf16[64,128]{1,0:T(8,128)(2,1)S(1)} %copy-done.3, f32[1,128]{1,0:T(1,128)S(1)} %bitcast.12, ...), custom_call_target="tpu_custom_call" | custom-call | tf_op jit(solution)/shard_map/pallas_call | solution.py:386
  43.8 0.6 %copy.48 = bf16[16,384]{1,0:T(8,128)(2,1)} copy(bf16[16,384]{1,0:T(8,128)(2,1)S(1)} %get-tuple-element.27) | data formatting | bytes 24576
  44.4 0.6 %copy.49 = f32[12,16]{1,0:T(8,128)} copy(f32[12,16]{1,0:T(8,128)S(1)} %get-tuple-element.28) | data formatting | bytes 1536
  (16 shorter events, 0.1 us)
Async XLA Ops:
  0.6 11.7 %copy-start = (bf16[2112,384]{1,0:T(8,128)(2,1)S(1)}, bf16[2112,384]{1,0:T(8,128)(2,1)}, u32[]{:S(2)}) copy-start(bf16[2112,384]{1,0:T(8,128)(2,1)} %w_out_h.1) | copy-start | bytes 4866052
  0.6 11.7 %copy-start.2 = (bf16[128,128]{1,0:T(8,128)(2,1)S(1)}, bf16[128,128]{1,0:T(8,128)(2,1)}, u32[]{:S(2)}) copy-start(bf16[128,128]{1,0:T(8,128)(2,1)} %w_pair_out.1) | copy-start | bytes 98308
  0.7 11.7 %copy-start.4 = (f32[128]{0:T(128)S(1)}, f32[128]{0:T(128)}, u32[]{:S(2)}) copy-start(f32[128]{0:T(128)} %param.31) | copy-start | bytes 1540
  0.7 11.7 %copy-start.3 = (bf16[64,128]{1,0:T(8,128)(2,1)S(1)}, bf16[64,128]{1,0:T(8,128)(2,1)}, u32[]{:S(2)}) copy-start(bf16[64,128]{1,0:T(8,128)(2,1)} %w_pair_in.1) | copy-start | bytes 49156
  0.7 11.7 %copy-start.1 = (bf16[384,384]{1,0:T(8,128)(2,1)S(1)}, bf16[384,384]{1,0:T(8,128)(2,1)}, u32[]{:S(2)}) copy-start(bf16[384,384]{1,0:T(8,128)(2,1)} %w_keyval_h.1) | copy-start | bytes 884740

commit v2 on v1

v2 whole, which is shorter than its diff:
```python
import functools

import jax
import jax.numpy as jnp
from jax import lax
from jax.experimental import pallas as pl
from jax.experimental.pallas import tpu as pltpu
from jax.sharding import PartitionSpec as P

F32 = jnp.float32
BF16 = jnp.bfloat16
MESH = pl.DeviceIdType.MESH
HP = 16
CHAINS = 8
AUX = 128


def dot(a, b):
    return jnp.dot(a, b, preferred_element_type=F32)


def dot_t(a, b):
    return lax.dot_general(a, b, (((1,), (1,)), ((), ())), preferred_element_type=F32)


def split3(x):
    hi = x.astype(BF16)
    rest = x - hi.astype(F32)
    mid = rest.astype(BF16)
    lo = (rest - mid.astype(F32)).astype(BF16)
    return hi, mid, lo


def onehot(mask):
    return jnp.where(mask, 1.0, 0.0).astype(BF16)


def iota(shape, dim):
    return lax.broadcasted_iota(jnp.int32, shape, dim)


def frame_columns(aux, base):
    wide = aux.astype(F32)
    return (
        wide[:, base : base + 12] + wide[:, base + 12 : base + 24] + wide[:, base + 24 : base + 36]
    )


def flip(index, other, size):
    if size & (size - 1):
        return (index + other) % size
    out = 0
    bit = 1
    while bit < size:
        out = out + ((index // bit + other // bit) % 2) * bit
        bit *= 2
    return out


def kernel(
    n, dims, single, angles, trans, left_factor, right_factor, chain, live, coef_in,
    w_pair_in, chain_bias, w_pair_out, w_bias, out_gain, w_frame, w_query, w_qpoints,
    w_keyval_h, w_kvpoints_h, w_out_h,
    single_out, frames_out,
    payload, left, gat, w_keyval, w_kvpoints, w_out, wk2, kv, kgk, kgv, ksq, wts, pair, attp, scale,
    win2, wout2, dead,
    send_sem, recv_sem, relay_sem, own_sem, w_sem, logit,
):
    heads, head_dim, qpts, vpts, rank, pair_dim = dims
    rows, cs = single_out.shape
    keys = n * rows
    width = heads * head_dim
    pts = qpts + vpts
    pw = heads * pts
    part = heads * qpts
    out_cols = heads * vpts
    fbase = rank + 3 * CHAINS
    third = (1.0 / 3.0) ** 0.5
    me = lax.axis_index("blk")
    chips = n // 2
    core = me % 2
    chip = me // 2
    sib = chip * 2 + 1 - core
    kb = 128
    group = kb // (2 * rows)
    blocks = keys // kb

    loads = [
        pltpu.make_async_copy(src, dst, w_sem.at[i])
        for i, (src, dst) in enumerate(
            [(w_keyval_h, w_keyval), (w_kvpoints_h, w_kvpoints), (w_out_h, w_out)]
        )
    ]
    barrier = pltpu.get_barrier_semaphore()

    def peer_of(d):
        return flip(chip, d, chips) * 2 + core

    def block(dev):
        return gat.at[pl.ds(pl.multiple_of(dev * rows, rows), rows), :]

    @pl.loop(1, chips)
    def _(d):
        pl.semaphore_signal(barrier, inc=1, device_id=(peer_of(d),), device_id_type=MESH)

    pl.semaphore_signal(barrier, inc=1, device_id=(sib,), device_id_type=MESH)
    for item in loads:
        item.start()

    cos, sin = jnp.cos(angles[...]), jnp.sin(angles[...])
    ca, cb, cc = cos[0:1], cos[1:2], cos[2:3]
    sa, sb, sc = sin[0:1], sin[1:2], sin[2:3]
    frame_rows = [
        ca * cb, -sa * cc + ca * sb * sc, sa * sc + ca * sb * cc,
        sa * cb, ca * cc + sa * sb * sc, -ca * sc + sa * sb * cc,
        -sb, cb * sc, cb * cc,
        trans[0:1, :], trans[1:2, :], trans[2:3, :],
    ]
    chain_row = chain[...].reshape(1, rows)
    live_row = live[...].reshape(1, rows).astype(F32)
    hot = jnp.where(iota((3 * CHAINS, rows), 0) % CHAINS == chain_row, 1.0, 0.0)
    frames = jnp.concatenate(frame_rows, axis=0)
    table = jnp.concatenate(
        [hot]
        + [item.astype(F32) for item in split3(frames)]
        + [live_row, jnp.zeros((AUX - fbase - 37, rows), F32)],
        axis=0,
    )
    side = AUX - rank
    table = jnp.concatenate([table, jnp.zeros((side, 128 - rows), F32)], axis=1).T[:rows]
    payload[:, :cs] = single[...]
    payload[:, cs:] = jnp.concatenate([right_factor[...].astype(F32), table], axis=1).astype(BF16)
    left[...] = jnp.concatenate(
        [left_factor[...].astype(F32), jnp.where(iota(table.shape, 1) < 3 * CHAINS, table, 0.0)],
        axis=1,
    )
    pl.semaphore_wait(barrier, chips)
    own = pltpu.make_async_copy(payload, block(me), own_sem)
    own.start()

    def send(dev):
        return pltpu.make_async_remote_copy(
            src_ref=payload, dst_ref=block(me), send_sem=send_sem.at[dev], recv_sem=recv_sem.at[me],
            device_id=(dev,), device_id_type=MESH,
        )

    def arrival(dev):
        return pltpu.make_async_remote_copy(
            src_ref=payload, dst_ref=block(dev), send_sem=send_sem.at[dev],
            recv_sem=recv_sem.at[dev], device_id=(sib,), device_id_type=MESH,
        )

    def relay(dev):
        return pltpu.make_async_remote_copy(
            src_ref=block(dev), dst_ref=block(dev), send_sem=relay_sem.at[dev],
            recv_sem=recv_sem.at[dev], device_id=(sib,), device_id_type=MESH,
        )

    send(sib).start()

    @pl.loop(1, chips)
    def _(d):
        send(peer_of(d)).start()

    own_x = single[...]
    own_frame = frame_columns(payload[:, cs:], fbase)
    query = dot_t(own_x, w_query[...]).astype(BF16).astype(F32)
    hrow = iota((rows, HP, width), 1)
    lane = iota((rows, HP, width), 2)
    vmask = ((lane >= hrow * head_dim) & (lane < (hrow + 1) * head_dim)).reshape(rows * HP, width)
    a_query = jnp.where(
        vmask, jnp.broadcast_to(query[:, None, :], (rows, HP, width)).reshape(rows * HP, width), 0.0
    ).astype(BF16)
    place = iota((128, part), 0)
    twice = onehot(
        (place == iota((128, part), 1)) | (place == iota((128, part), 1) + part)
    )
    qp = [
        dot_t(own_x, dot(twice, w_qpoints[y * part : (y + 1) * part, :]).astype(BF16))
        for y in range(3)
    ]
    hrow = iota((rows, HP, 128), 1)
    lane = iota((rows, HP, 128), 2)
    mask_hi = ((lane >= hrow * qpts) & (lane < (hrow + 1) * qpts)).reshape(rows * HP, 128)
    mask_mid = (
        (lane >= part + hrow * qpts) & (lane < part + (hrow + 1) * qpts)
    ).reshape(rows * HP, 128)
    amask = ((lane >= hrow * vpts) & (lane < (hrow + 1) * vpts)).reshape(rows * HP, 128)
    a_first, a_last = [], []
    qsum = 0.0
    for x in range(3):
        point = own_frame[:, 9 + x : 10 + x]
        for y in range(3):
            point = point + own_frame[:, 3 * x + y : 3 * x + y + 1] * qp[y]
        point = jnp.broadcast_to(point[:, None, :], (rows, HP, 128)).reshape(rows * HP, 128)
        only = jnp.where(mask_hi, point, 0.0)
        qsum = qsum + only * only
        hi, mid, lo = [item.astype(F32) for item in split3(point)]
        a_first.append(jnp.where(mask_hi, hi, jnp.where(mask_mid, mid, 0.0)).astype(BF16))
        a_last.append(jnp.where(mask_hi, lo, 0.0).astype(BF16))
    a_first = jnp.concatenate(a_first, axis=1)
    a_last = jnp.concatenate(a_last, axis=1)
    qsq = jnp.sum(qsum, axis=1, keepdims=True)
    diag = iota((HP, heads), 0) == iota((HP, heads), 1)
    factor = (2.0 / (9.0 * qpts)) ** 0.5 / 2.0
    coef16 = jnp.sum(
        jnp.where(diag, coef_in[...].reshape(1, heads) * factor, 0.0), axis=1, keepdims=True
    )
    coef = jnp.broadcast_to(coef16[None], (rows, HP, 1)).reshape(rows * HP, 1)

    def twin(block_w):
        none = jnp.zeros(block_w.shape, block_w.dtype)
        return jnp.concatenate(
            [
                jnp.concatenate([block_w, none], axis=1),
                jnp.concatenate([none, block_w], axis=1),
            ],
            axis=0,
        )

    bias_parts = [
        jnp.broadcast_to(item.astype(F32), (CHAINS, pair_dim))
        for item in split3(chain_bias[...].reshape(1, pair_dim))
    ]
    win2[...] = twin(
        jnp.concatenate(
            [w_pair_in[...].astype(F32)] + bias_parts + [jnp.zeros((AUX - fbase, pair_dim), F32)],
            axis=0,
        ).astype(BF16)
    )
    w_o = w_pair_out[...].astype(F32)
    w_o = w_o - jnp.mean(w_o, axis=1, keepdims=True)
    w_hi = w_o.astype(BF16)
    wout2[0] = twin(w_hi)
    wout2[1] = twin((w_o - w_hi.astype(F32)).astype(BF16))
    wout2[2] = twin(jnp.full((pair_dim, pair_dim), 1.0 / pair_dim, BF16))
    w_b2 = twin(dot(onehot(diag), w_bias[...]).astype(BF16))

    loads[0].wait()
    loads[1].wait()
    place = iota((256, pw), 0)
    source = iota((256, pw), 1)
    kcol = (source // pts) * qpts + source % pts
    vcol = 128 + (source // pts) * vpts + source % pts - qpts
    is_key = source % pts < qpts
    order = onehot(
        (is_key & ((place == kcol) | (place == kcol + part))) | ((source % pts >= qpts) & (place == vcol))
    )
    for y in range(3):
        wk2[y * 256 : (y + 1) * 256, :] = dot(
            order, w_kvpoints[y * pw : (y + 1) * pw, :]
        ).astype(BF16)

    hrow = iota((HP, 128), 0)
    lane = iota((HP, 128), 1)
    hsel = onehot((lane >= hrow * qpts) & (lane < (hrow + 1) * qpts))
    live_sel = onehot(iota((HP, AUX), 1) == fbase + 36)

    def forward(k, first):
        @pl.loop(first, group)
        def _(j):
            dev = peer_of(k * group + j)
            arrival(dev).wait_recv()
            relay(dev).start()

    def settle(k, first):
        @pl.loop(first, group)
        def _(j):
            arrival(flip(chip, k * group + j, chips) * 2 + 1 - core).wait_recv()

    forward(0, 1)
    own.wait()
    arrival(sib).wait_recv()
    settle(0, 1)

    @pl.loop(0, blocks)
    def _(k):
        base = flip(chip // group, k, blocks) * kb
        at = pl.ds(pl.multiple_of(base, kb), kb)
        x_in = gat[at, :cs]
        aux = gat[at, cs:]
        kv[at, :] = dot(x_in, w_keyval[...]).astype(BF16)
        kp = dot_t(x_in, wk2[...])
        frame = frame_columns(aux, fbase)
        square = 0.0
        for x in range(3):
            point = frame[:, 9 + x : 10 + x]
            for y in range(3):
                point = point + frame[:, 3 * x + y : 3 * x + y + 1] * kp[:, y * 256 : (y + 1) * 256]
            point = point.astype(BF16)
            kgk[at, x * 128 : (x + 1) * 128] = point[:, :128]
            kgv[at, x * 128 : (x + 1) * 128] = point[:, 128:]
            wide = point[:, :128].astype(F32)
            square = square + wide * wide
        total = 0.0
        for item in split3(square):
            total = total + dot_t(hsel, item)
        ksq[:, at] = total
        dead[:, at] = 100000.0 * (1.0 - dot_t(live_sel, aux))

        @pl.when(k + 1 < blocks)
        def _():
            forward(k + 1, 0)

        @pl.loop(0, rows // 2, unroll=2)
        def _(t):
            right = aux.astype(F32)
            prod = jnp.concatenate(
                [
                    (right * left[pl.ds(2 * t, 1), :]).astype(BF16),
                    (right * left[pl.ds(2 * t + 1, 1), :]).astype(BF16),
                ],
                axis=1,
            )
            hidden = dot(prod, win2[...])
            hidden = jax.nn.gelu(hidden, approximate=True).astype(BF16)
            center = dot(hidden, wout2[0]) + dot(hidden, wout2[1])
            for half in range(2):
                o = center[:, half * pair_dim : (half + 1) * pair_dim]
                var = jnp.mean(o * o, axis=1, keepdims=True)
                pair[t, at, half * pair_dim : (half + 1) * pair_dim] = (
                    o * lax.rsqrt(var + 1e-05)
                ).astype(BF16)

        @pl.when(k + 1 < blocks)
        def _():
            settle(k + 1, 0)

    both_dead = jnp.concatenate([dead[...], dead[...]], axis=0)
    kstep = 512 if keys % 512 == 0 else kb

    @pl.loop(0, keys // kstep)
    def _(b):
        at = pl.ds(pl.multiple_of(b * kstep, kstep), kstep)
        near = kgk[at, :]
        cross = dot_t(a_first, near) + dot_t(a_last, near)
        scalar = dot_t(a_query, kv[at, :width]) * head_dim ** (-0.5)
        square = jnp.broadcast_to(ksq[:, at][None], (rows, HP, kstep)).reshape(rows * HP, kstep)
        logit[:, at] = scalar - coef * (qsq + square - 2.0 * cross)

    @pl.loop(0, rows // 2, unroll=2)
    def _(t):
        sel = pl.ds(pl.multiple_of(t * 2 * HP, 2 * HP), 2 * HP)
        both = pair[t]
        bias = dot_t(w_b2, both)
        row = third * (logit[sel, :] + bias) - both_dead
        top = jnp.max(row, axis=1, keepdims=True)
        terms = jnp.exp(row - top)
        inv = 1.0 / jnp.sum(terms, axis=1, keepdims=True)
        weight = terms.astype(BF16)
        wts[sel, :] = weight
        scale[sel, :] = jnp.broadcast_to(inv, (2 * HP, 128))
        out = dot(weight, both) * inv
        attp[sel, :] = jnp.concatenate([out[:HP, :pair_dim], out[HP:, pair_dim:]], axis=0)

    weight = wts[...]
    inv = scale[:, :1]

    def pick(value, mask):
        value = jnp.where(mask, value * inv, 0.0)
        return jnp.sum(value.reshape(rows, HP, value.shape[1]), axis=1)

    values = pick(dot(weight, kv[:, width:]), vmask)
    points = dot(weight, kgv[...])
    away = [
        pick(points[:, y * 128 : (y + 1) * 128], amask) - own_frame[:, 9 + y : 10 + y]
        for y in range(3)
    ]
    loads[2].wait()
    mixed = own_x.astype(F32) + dot(values.astype(BF16), w_out[:width, :])
    norm = 0.0
    for x in range(3):
        local = 0.0
        for y in range(3):
            local = local + own_frame[:, 3 * y + x : 3 * y + x + 1] * away[y]
        norm = norm + local * local
        first = width + x * out_cols
        mixed = mixed + dot(local[:, :out_cols].astype(BF16), w_out[first : first + out_cols, :])
    first = width + 3 * out_cols
    item = jnp.sqrt(norm + 1e-08)[:, :out_cols].astype(BF16)
    mixed = mixed + dot(item, w_out[first : first + out_cols, :])
    first = first + out_cols
    for h in range(heads):
        item = attp[pl.ds(h, rows, stride=HP), :].astype(BF16)
        mixed = mixed + dot(item, w_out[first + h * pair_dim : first + (h + 1) * pair_dim, :])

    center = mixed - jnp.mean(mixed, axis=1, keepdims=True)
    var = jnp.mean(center * center, axis=1, keepdims=True)
    snew = center * lax.rsqrt(var + 1e-05) * out_gain[...].reshape(1, cs)
    single_out[...] = snew.astype(BF16)
    update = lax.dot_general(
        w_frame[...], snew, (((1,), (1,)), ((), ())),
        precision=lax.Precision.HIGHEST, preferred_element_type=F32,
    )
    b, c, d = update[0:1], update[1:2], update[2:3]
    size = jnp.sqrt(1.0 + b * b + c * c + d * d)
    a = 1.0 / size
    b, c, d = b / size, c / size, d / size
    ru = [
        [a * a + b * b - c * c - d * d, 2.0 * (b * c - a * d), 2.0 * (b * d + a * c)],
        [2.0 * (b * c + a * d), a * a - b * b + c * c - d * d, 2.0 * (c * d - a * b)],
        [2.0 * (b * d - a * c), 2.0 * (c * d + a * b), a * a - b * b - c * c + d * d],
    ]
    for x in range(3):
        r0, r1, r2 = frame_rows[3 * x : 3 * x + 3]
        for z in range(3):
            frames_out[3 * x + z : 3 * x + z + 1, :] = r0 * ru[0][z] + r1 * ru[1][z] + r2 * ru[2][z]
        frames_out[9 + x : 10 + x, :] = (
            r0 * update[3:4] + r1 * update[4:5] + r2 * update[5:6] + frame_rows[9 + x]
        )

    @pl.loop(1, chips)
    def _(d):
        dev = peer_of(d)
        send(dev).wait_send()
        relay(dev).wait_send()

    send(sib).wait_send()


def per_device(
    n, single, angles, trans, left_factor, right_factor, chain, live, w_query, w_keyval, w_qpoints,
    w_kvpoints, w_pair_in, chain_bias, w_pair_out, w_bias, point_weight, w_out, out_gain, w_frame,
):
    rows, cs = single.shape
    heads = point_weight.shape[0]
    head_dim = w_query.shape[1] // heads
    qpts = w_qpoints.shape[1] // (3 * heads)
    vpts = w_kvpoints.shape[1] // (3 * heads) - qpts
    rank, pair_dim = w_pair_in.shape
    keys = n * rows
    vmem = pl.BlockSpec(memory_space=pltpu.VMEM)
    hbm = pl.BlockSpec(memory_space=pltpu.HBM)
    return pl.pallas_call(
        functools.partial(kernel, n, (heads, head_dim, qpts, vpts, rank, pair_dim)),
        out_shape=(
            jax.ShapeDtypeStruct((rows, cs), BF16),
            jax.ShapeDtypeStruct((12, rows), F32),
        ),
        in_specs=[vmem] * 16 + [hbm] * 3,
        out_specs=(vmem, vmem),
        scratch_shapes=[
            pltpu.VMEM((rows, cs + AUX), BF16),
            pltpu.VMEM((rows, AUX), F32),
            pltpu.VMEM((keys, cs + AUX), BF16),
            pltpu.VMEM(w_keyval.shape, BF16),
            pltpu.VMEM(w_kvpoints.shape[::-1], BF16),
            pltpu.VMEM(w_out.shape, BF16),
            pltpu.VMEM((3 * 256, cs), BF16),
            pltpu.VMEM((keys, w_keyval.shape[1]), BF16),
            pltpu.VMEM((keys, 3 * 128), BF16),
            pltpu.VMEM((keys, 3 * 128), BF16),
            pltpu.VMEM((HP, keys), F32),
            pltpu.VMEM((rows * HP, keys), BF16),
            pltpu.VMEM((rows // 2, keys, 2 * pair_dim), BF16),
            pltpu.VMEM((rows * HP, pair_dim), F32),
            pltpu.VMEM((rows * HP, 128), F32),
            pltpu.VMEM((2 * AUX, 2 * pair_dim), BF16),
            pltpu.VMEM((3, 2 * pair_dim, 2 * pair_dim), BF16),
            pltpu.VMEM((HP, keys), F32),
            pltpu.SemaphoreType.DMA((n,)),
            pltpu.SemaphoreType.DMA((n,)),
            pltpu.SemaphoreType.DMA((n,)),
            pltpu.SemaphoreType.DMA,
            pltpu.SemaphoreType.DMA((3,)),
            pltpu.VMEM((rows * HP, keys), F32),
        ],
        compiler_params=pltpu.CompilerParams(
            collective_id=0, has_side_effects=True, vmem_limit_bytes=50 * 1024 * 1024
        ),
    )(
        single, angles, trans, left_factor, right_factor, chain, live, point_weight,
        w_pair_in, chain_bias, w_pair_out, w_bias.T, out_gain, w_frame.T, w_query.T, w_qpoints.T,
        w_keyval, w_kvpoints.T, w_out,
    )


def solution(mesh):
    row = P("blk", None)
    col = P(None, "blk")
    in_specs = (row, col, col, row, row, P("blk"), P("blk")) + (P(),) * 12
    return jax.shard_map(
        functools.partial(per_device, mesh.shape["blk"]),
        mesh=mesh, in_specs=in_specs, out_specs=(row, col), check_vma=False,
    )
```

time: 45.9 us -> 45.4 us (0.989)
  local copies, waits for them, and re-layouts: 10.6 us -> 16 us
  Pallas kernels: 31.5 us -> 28.1 us
  other arithmetic: 2.2 us -> 0 us
    unnamed x21 -> x40, local copies, waits for them, and re-layouts: 7.11 us -> 16 us
    pallas_call x1, Pallas kernels: 31.5 us -> 28.1 us  [per_device(): pl.pallas_call(functools.partial(kernel, n, (heads, head_dim, qpts, vpts,...]
    concatenate x2 -> x0, local copies, waits for them, and re-layouts: 1.58 us -> none  [the longest x1 0.8 us: per_device(): jnp.concatenate([single, right_factor, hot, hot, hot] + [item.astype(BF16...]
    broadcast_in_dim x6 -> x0, local copies, waits for them, and re-layouts: 0.87 us -> none  [the longest x1 0.68 us: per_device(): out_gain[None, :]]
    slice x1 -> x0, local copies, waits for them, and re-layouts: 0.8 us -> none  [rotation(): cc, sc = (jnp.cos(angles[2]), jnp.sin(angles[2]))]
    broadcast_in_dim x1 -> x0, other arithmetic: 0.79 us -> none  [per_device(): live.astype(BF16)[:, None]]
    convert_element_type x3 -> x0, other arithmetic: 0.74 us -> none  [the longest x1 0.73 us: per_device(): hot = (chain[:, None] == jnp.arange(CHAINS)[None, :]).astype(BF16)]
    div x1 -> x0, other arithmetic: 0.66 us -> none  [per_device(): point_weight * (2.0 / (9.0 * qpts)) ** 0.5 / 2.0]
where the time goes in v2:
time: 45.4 us; the launch traced here: 44.8 us
  Pallas kernels  28.1 us (62%)
  local copies, waits for them, and re-layouts  16 us (35%)
  between operations  0.67 us (1%)
    pallas_call x1, Pallas kernels, per_device(): pl.pallas_call(functools.partial(kernel, n, (heads, head_dim, qpts, vpts,...  28.1 us
    unnamed x40, local copies, waits for them, and re-layouts  16 us

profile of v2, /device:TPU:1, one launch (start us, length us, event | category | flops | bytes accessed | tf_op | source)
XLA Modules:
  0.0 44.8 jit_solution(15740629741146400615)
XLA Ops:
  0.6 0.0 copy-start
  0.6 1.4 %copy-done = bf16[2112,384]{1,0:T(8,128)(2,1)S(1)} copy-done((bf16[2112,384]{1,0:T(8,128)(2,1)S(1)}, bf16[2112,384]{1,0:T(8,128)(2,1)}, u32[]{:S(2)}) %copy-start) | copy-done | bytes 1622040
  2.1 0.0 copy-start.1
  2.1 1.0 %copy-done.1 = bf16[384,432]{0,1:T(8,128)(2,1)S(1)} copy-done((bf16[384,432]{0,1:T(8,128)(2,1)S(1)}, bf16[384,432]{0,1:T(8,128)(2,1)}, u32[]{:S(2)}) %copy-start.1) | copy-done | bytes 331800
  3.0 1.0 %copy-done.2 = bf16[384,384]{1,0:T(8,128)(2,1)S(1)} copy-done((bf16[384,384]{1,0:T(8,128)(2,1)S(1)}, bf16[384,384]{1,0:T(8,128)(2,1)}, u32[]{:S(2)}) %copy-start.2) | copy-done | bytes 294936
  4.0 0.9 %copy-done.3 = bf16[384,192]{0,1:T(8,128)(2,1)S(1)} copy-done((bf16[384,192]{0,1:T(8,128)(2,1)S(1)}, bf16[384,192]{0,1:T(8,128)(2,1)}, u32[]{:S(2)}) %copy-start.3) | copy-done | bytes 147480
  4.9 0.9 %copy-done.4 = bf16[384,144]{0,1:T(8,128)(2,1)S(1)} copy-done((bf16[384,144]{0,1:T(8,128)(2,1)S(1)}, bf16[384,144]{0,1:T(8,128)(2,1)}, u32[]{:S(2)}) %copy-start.4) | copy-done | bytes 110616
  5.8 0.8 %copy-done.5 = bf16[128,128]{1,0:T(8,128)(2,1)S(1)} copy-done((bf16[128,128]{1,0:T(8,128)(2,1)S(1)}, bf16[128,128]{1,0:T(8,128)(2,1)}, u32[]{:S(2)}) %copy-start.5) | copy-done | bytes 32792
  6.6 0.7 %copy-done.6 = bf16[64,128]{1,0:T(8,128)(2,1)S(1)} copy-done((bf16[64,128]{1,0:T(8,128)(2,1)S(1)}, bf16[64,128]{1,0:T(8,128)(2,1)}, u32[]{:S(2)}) %copy-start.6) | copy-done | bytes 16408
  7.3 0.7 %copy-done.7 = bf16[16,384]{1,0:T(8,128)(2,1)S(1)} copy-done((bf16[16,384]{1,0:T(8,128)(2,1)S(1)}, bf16[16,384]{1,0:T(8,128)(2,1)}, u32[]{:S(2)}) %copy-start.7) | copy-done | bytes 12312
  8.0 0.7 %copy-done.8 = f32[384,6]{0,1:T(8,128)S(1)} copy-done((f32[384,6]{0,1:T(8,128)S(1)}, f32[384,6]{0,1:T(8,128)}, u32[]{:S(2)}) %copy-start.8) | copy-done | bytes 9240
  8.7 0.7 %copy-done.9 = bf16[16,64]{1,0:T(8,128)(2,1)S(1)} copy-done((bf16[16,64]{1,0:T(8,128)(2,1)S(1)}, bf16[16,64]{1,0:T(8,128)(2,1)}, u32[]{:S(2)}) %copy-start.9) | copy-done | bytes 2072
  9.4 0.7 %copy-done.10 = bf16[16,64]{1,0:T(8,128)(2,1)S(1)} copy-done((bf16[16,64]{1,0:T(8,128)(2,1)S(1)}, bf16[16,64]{1,0:T(8,128)(2,1)}, u32[]{:S(2)}) %copy-start.10) | copy-done | bytes 2072
  10.1 0.7 %copy-done.11 = bf16[128,12]{0,1:T(8,128)(2,1)S(1)} copy-done((bf16[128,12]{0,1:T(8,128)(2,1)S(1)}, bf16[128,12]{0,1:T(8,128)(2,1)}, u32[]{:S(2)}) %copy-start.11) | copy-done | bytes 3096
  10.8 0.7 %copy-done.12 = f32[3,16]{1,0:T(4,128)S(1)} copy-done((f32[3,16]{1,0:T(4,128)S(1)}, f32[3,16]{1,0:T(4,128)}, u32[]{:S(2)}) %copy-start.12) | copy-done | bytes 216
  11.4 0.7 %copy-done.13 = f32[3,16]{1,0:T(4,128)S(1)} copy-done((f32[3,16]{1,0:T(4,128)S(1)}, f32[3,16]{1,0:T(4,128)}, u32[]{:S(2)}) %copy-start.13) | copy-done | bytes 216
  12.1 0.7 %copy-done.14 = f32[384]{0:T(512)S(1)} copy-done((f32[384]{0:T(512)S(1)}, f32[384]{0:T(512)}, u32[]{:S(2)}) %copy-start.14) | copy-done | bytes 1560
  12.8 0.7 %copy-done.15 = s32[16]{0:T(128)S(1)} copy-done((s32[16]{0:T(128)S(1)}, s32[16]{0:T(128)}, u32[]{:S(2)}) %copy-start.15) | copy-done | bytes 88
  13.5 0.7 %copy-done.16 = s32[16]{0:T(128)S(1)} copy-done((s32[16]{0:T(128)S(1)}, s32[16]{0:T(128)}, u32[]{:S(2)}) %copy-start.16) | copy-done | bytes 88
  14.1 0.7 %copy-done.17 = f32[12]{0:T(128)S(1)} copy-done((f32[12]{0:T(128)S(1)}, f32[12]{0:T(128)}, u32[]{:S(2)}) %copy-start.17) | copy-done | bytes 72
  14.8 0.7 %copy-done.18 = f32[128]{0:T(128)S(1)} copy-done((f32[128]{0:T(128)S(1)}, f32[128]{0:T(128)}, u32[]{:S(2)}) %copy-start.18) | copy-done | bytes 536
  15.4 28.1 %shard_map.194 = (bf16[16,384]{1,0:T(8,128)(2,1)S(1)}, f32[12,16]{1,0:T(8,128)S(1)}) custom-call(bf16[16,384]{1,0:T(8,128)(2,1)S(1)} %copy-done.7, f32[3,16]{1,0:T(4,128)S(1)} %copy-done.12, f32[3,16]{1,0:T(4,128)S(1)} %copy-done.13, bf16[16,64]{1,0:T(8,128)(2,1)S(1)} %copy-done.9, bf16[16,64]{1,0:T(8,128)(2,1)S(1)} %copy-done.10, s32[16]{0:T(128)S(1)} %copy-done.15, ...), custom_call_target="tpu_custom_call" | custom-call | tf_op jit(solution)/shard_map/pallas_call | solution.py:434
  43.6 0.6 %copy.23 = bf16[16,384]{1,0:T(8,128)(2,1)} copy(bf16[16,384]{1,0:T(8,128)(2,1)S(1)} %get-tuple-element.4) | data formatting | bytes 24576
  44.2 0.6 %copy.24 = f32[12,16]{1,0:T(8,128)} copy(f32[12,16]{1,0:T(8,128)S(1)} %get-tuple-element.5) | data formatting | bytes 1536
  (17 shorter events, 0.0 us)
Async XLA Ops:
  0.6 1.4 %copy-start = (bf16[2112,384]{1,0:T(8,128)(2,1)S(1)}, bf16[2112,384]{1,0:T(8,128)(2,1)}, u32[]{:S(2)}) copy-start(bf16[2112,384]{1,0:T(8,128)(2,1)} %w_out_h.1) | copy-start | bytes 4866052
  2.1 1.0 %copy-start.1 = (bf16[384,432]{0,1:T(8,128)(2,1)S(1)}, bf16[384,432]{0,1:T(8,128)(2,1)}, u32[]{:S(2)}) copy-start(bf16[384,432]{0,1:T(8,128)(2,1)} %param.29) | copy-start | bytes 995332
  3.0 1.0 %copy-start.2 = (bf16[384,384]{1,0:T(8,128)(2,1)S(1)}, bf16[384,384]{1,0:T(8,128)(2,1)}, u32[]{:S(2)}) copy-start(bf16[384,384]{1,0:T(8,128)(2,1)} %w_keyval_h.1) | copy-start | bytes 884740
  4.0 0.9 %copy-start.3 = (bf16[384,192]{0,1:T(8,128)(2,1)S(1)}, bf16[384,192]{0,1:T(8,128)(2,1)}, u32[]{:S(2)}) copy-start(bf16[384,192]{0,1:T(8,128)(2,1)} %param.26) | copy-start | bytes 442372
  4.9 0.9 %copy-start.4 = (bf16[384,144]{0,1:T(8,128)(2,1)S(1)}, bf16[384,144]{0,1:T(8,128)(2,1)}, u32[]{:S(2)}) copy-start(bf16[384,144]{0,1:T(8,128)(2,1)} %param.28) | copy-start | bytes 331780
  5.8 0.8 %copy-start.5 = (bf16[128,128]{1,0:T(8,128)(2,1)S(1)}, bf16[128,128]{1,0:T(8,128)(2,1)}, u32[]{:S(2)}) copy-start(bf16[128,128]{1,0:T(8,128)(2,1)} %w_pair_out.1) | copy-start | bytes 98308
  6.6 0.7 %copy-start.6 = (bf16[64,128]{1,0:T(8,128)(2,1)S(1)}, bf16[64,128]{1,0:T(8,128)(2,1)}, u32[]{:S(2)}) copy-start(bf16[64,128]{1,0:T(8,128)(2,1)} %w_pair_in.1) | copy-start | bytes 49156
  7.3 0.7 %copy-start.7 = (bf16[16,384]{1,0:T(8,128)(2,1)S(1)}, bf16[16,384]{1,0:T(8,128)(2,1)}, u32[]{:S(2)}) copy-start(bf16[16,384]{1,0:T(8,128)(2,1)} %single.1) | copy-start | bytes 36868
  8.0 0.7 %copy-start.8 = (f32[384,6]{0,1:T(8,128)S(1)}, f32[384,6]{0,1:T(8,128)}, u32[]{:S(2)}) copy-start(f32[384,6]{0,1:T(8,128)} %param.37) | copy-start | bytes 27652
  8.7 0.7 %copy-start.9 = (bf16[16,64]{1,0:T(8,128)(2,1)S(1)}, bf16[16,64]{1,0:T(8,128)(2,1)}, u32[]{:S(2)}) copy-start(bf16[16,64]{1,0:T(8,128)(2,1)} %left_factor.1) | copy-start | bytes 6148
  9.4 0.7 %copy-start.10 = (bf16[16,64]{1,0:T(8,128)(2,1)S(1)}, bf16[16,64]{1,0:T(8,128)(2,1)}, u32[]{:S(2)}) copy-start(bf16[16,64]{1,0:T(8,128)(2,1)} %right_factor.1) | copy-start | bytes 6148
  10.1 0.7 %copy-start.11 = (bf16[128,12]{0,1:T(8,128)(2,1)S(1)}, bf16[128,12]{0,1:T(8,128)(2,1)}, u32[]{:S(2)}) copy-start(bf16[128,12]{0,1:T(8,128)(2,1)} %param.33) | copy-start | bytes 9220
  10.8 0.7 %copy-start.12 = (f32[3,16]{1,0:T(4,128)S(1)}, f32[3,16]{1,0:T(4,128)}, u32[]{:S(2)}) copy-start(f32[3,16]{1,0:T(4,128)} %angles.1) | copy-start | bytes 580
  11.4 0.7 %copy-start.13 = (f32[3,16]{1,0:T(4,128)S(1)}, f32[3,16]{1,0:T(4,128)}, u32[]{:S(2)}) copy-start(f32[3,16]{1,0:T(4,128)} %trans.1) | copy-start | bytes 580
  12.1 0.7 %copy-start.14 = (f32[384]{0:T(512)S(1)}, f32[384]{0:T(512)}, u32[]{:S(2)}) copy-start(f32[384]{0:T(512)} %out_gain.1) | copy-start | bytes 4612
  12.8 0.7 %copy-start.15 = (s32[16]{0:T(128)S(1)}, s32[16]{0:T(128)}, u32[]{:S(2)}) copy-start(s32[16]{0:T(128)} %chain.1) | copy-start | bytes 196
  13.5 0.7 %copy-start.16 = (s32[16]{0:T(128)S(1)}, s32[16]{0:T(128)}, u32[]{:S(2)}) copy-start(s32[16]{0:T(128)} %live.1) | copy-start | bytes 196
  14.1 0.7 %copy-start.17 = (f32[12]{0:T(128)S(1)}, f32[12]{0:T(128)}, u32[]{:S(2)}) copy-start(f32[12]{0:T(128)} %coef_in.1) | copy-start | bytes 148
  14.8 0.7 %copy-start.18 = (f32[128]{0:T(128)S(1)}, f32[128]{0:T(128)}, u32[]{:S(2)}) copy-start(f32[128]{0:T(128)} %chain_bias.1) | copy-start | bytes 1540

commit v3 on v2

--- a/solution.py
+++ b/solution.py
@@ -58,14 +58,20 @@
 
 
 def kernel(
-    n, dims, single, angles, trans, left_factor, right_factor, chain, live, coef_in,
-    w_pair_in, chain_bias, w_pair_out, w_bias, out_gain, w_frame, w_query, w_qpoints,
-    w_keyval_h, w_kvpoints_h, w_out_h,
-    single_out, frames_out,
-    payload, left, gat, w_keyval, w_kvpoints, w_out, wk2, kv, kgk, kgv, ksq, wts, pair, attp, scale,
-    win2, wout2, dead,
-    send_sem, recv_sem, relay_sem, own_sem, w_sem, logit,
+    n, dims, *refs,
 ):
+    sources = refs[:19]
+    single_out, frames_out = refs[19:21]
+    held = refs[21:40]
+    (
+        payload, left, gat, wk2, kv, kgk, kgv, ksq, wts, pair, attp, scale, win2, wout2, dead,
+        send_sem, recv_sem, relay_sem, own_sem, w_sem, logit, bias_rows,
+    ) = refs[40:]
+    (
+        single, angles, trans, left_factor, right_factor, chain, live, coef_in, w_pair_in,
+        chain_bias, w_pair_out, w_bias, out_gain, w_frame, w_query, w_qpoints, w_keyval,
+        w_kvpoints, w_out,
+    ) = held
     heads, head_dim, qpts, vpts, rank, pair_dim = dims
     rows, cs = single_out.shape
     keys = n * rows
@@ -87,10 +93,10 @@
 
     loads = [
         pltpu.make_async_copy(src, dst, w_sem.at[i])
-        for i, (src, dst) in enumerate(
-            [(w_keyval_h, w_keyval), (w_kvpoints_h, w_kvpoints), (w_out_h, w_out)]
-        )
-    ]
+        for i, (src, dst) in enumerate(zip(sources, held))
+    ]
+    for item in loads:
+        item.start()
     barrier = pltpu.get_barrier_semaphore()
 
     def peer_of(d):
@@ -104,8 +110,8 @@
         pl.semaphore_signal(barrier, inc=1, device_id=(peer_of(d),), device_id_type=MESH)
 
     pl.semaphore_signal(barrier, inc=1, device_id=(sib,), device_id_type=MESH)
-    for item in loads:
-        item.start()
+    for item in loads[:7]:
+        item.wait()
 
     cos, sin = jnp.cos(angles[...]), jnp.sin(angles[...])
     ca, cb, cc = cos[0:1], cos[1:2], cos[2:3]
@@ -162,6 +168,8 @@
     def _(d):
         send(peer_of(d)).start()
 
+    for item in loads[7:16]:
+        item.wait()
     own_x = single[...]
     own_frame = frame_columns(payload[:, cs:], fbase)
     query = dot_t(own_x, w_query[...]).astype(BF16).astype(F32)
@@ -236,8 +244,8 @@
     wout2[2] = twin(jnp.full((pair_dim, pair_dim), 1.0 / pair_dim, BF16))
     w_b2 = twin(dot(onehot(diag), w_bias[...]).astype(BF16))
 
-    loads[0].wait()
-    loads[1].wait()
+    loads[16].wait()
+    loads[17].wait()
     place = iota((256, pw), 0)
     source = iota((256, pw), 1)
     kcol = (source // pts) * qpts + source % pts
@@ -315,12 +323,15 @@
             hidden = dot(prod, win2[...])
             hidden = jax.nn.gelu(hidden, approximate=True).astype(BF16)
             center = dot(hidden, wout2[0]) + dot(hidden, wout2[1])
+            normed = []
             for half in range(2):
                 o = center[:, half * pair_dim : (half + 1) * pair_dim]
                 var = jnp.mean(o * o, axis=1, keepdims=True)
-                pair[t, at, half * pair_dim : (half + 1) * pair_dim] = (
-                    o * lax.rsqrt(var + 1e-05)
-                ).astype(BF16)
+                normed.append((o * lax.rsqrt(var + 1e-05)).astype(BF16))
+            normed = jnp.concatenate(normed, axis=1)
+            pair[t, at, :] = normed
+            sel = pl.ds(pl.multiple_of(t * 2 * HP, 2 * HP), 2 * HP)
+            bias_rows[sel, at] = dot_t(w_b2, normed)
 
         @pl.when(k + 1 < blocks)
         def _():
@@ -338,12 +349,11 @@
         square = jnp.broadcast_to(ksq[:, at][None], (rows, HP, kstep)).reshape(rows * HP, kstep)
         logit[:, at] = scalar - coef * (qsq + square - 2.0 * cross)
 
-    @pl.loop(0, rows // 2, unroll=2)
+    @pl.loop(0, rows // 2, unroll=4)
     def _(t):
         sel = pl.ds(pl.multiple_of(t * 2 * HP, 2 * HP), 2 * HP)
         both = pair[t]
-        bias = dot_t(w_b2, both)
-        row = third * (logit[sel, :] + bias) - both_dead
+        row = third * (logit[sel, :] + bias_rows[sel, :]) - both_dead
         top = jnp.max(row, axis=1, keepdims=True)
         terms = jnp.exp(row - top)
         inv = 1.0 / jnp.sum(terms, axis=1, keepdims=True)
@@ -366,7 +376,7 @@
         pick(points[:, y * 128 : (y + 1) * 128], amask) - own_frame[:, 9 + y : 10 + y]
         for y in range(3)
     ]
-    loads[2].wait()
+    loads[18].wait()
     mixed = own_x.astype(F32) + dot(values.astype(BF16), w_out[:width, :])
     norm = 0.0
     for x in range(3):
@@ -431,21 +441,23 @@
     keys = n * rows
     vmem = pl.BlockSpec(memory_space=pltpu.VMEM)
     hbm = pl.BlockSpec(memory_space=pltpu.HBM)
+    args = (
+        single, angles, trans, left_factor, right_factor, chain, live, point_weight,
+        w_pair_in, chain_bias, w_pair_out, w_bias.T, out_gain, w_frame.T, w_query.T, w_qpoints.T,
+        w_keyval, w_kvpoints.T, w_out,
+    )
     return pl.pallas_call(
         functools.partial(kernel, n, (heads, head_dim, qpts, vpts, rank, pair_dim)),
         out_shape=(
             jax.ShapeDtypeStruct((rows, cs), BF16),
             jax.ShapeDtypeStruct((12, rows), F32),
         ),
-        in_specs=[vmem] * 16 + [hbm] * 3,
+        in_specs=[hbm] * len(args),
         out_specs=(vmem, vmem),
-        scratch_shapes=[
+        scratch_shapes=[pltpu.VMEM(item.shape, item.dtype) for item in args] + [
             pltpu.VMEM((rows, cs + AUX), BF16),
             pltpu.VMEM((rows, AUX), F32),
             pltpu.VMEM((keys, cs + AUX), BF16),
-            pltpu.VMEM(w_keyval.shape, BF16),
-            pltpu.VMEM(w_kvpoints.shape[::-1], BF16),
-            pltpu.VMEM(w_out.shape, BF16),
             pltpu.VMEM((3 * 256, cs), BF16),
             pltpu.VMEM((keys, w_keyval.shape[1]), BF16),
             pltpu.VMEM((keys, 3 * 128), BF16),
@@ -462,17 +474,14 @@
             pltpu.SemaphoreType.DMA((n,)),
             pltpu.SemaphoreType.DMA((n,)),
             pltpu.SemaphoreType.DMA,
-            pltpu.SemaphoreType.DMA((3,)),
+            pltpu.SemaphoreType.DMA((len(args),)),
+            pltpu.VMEM((rows * HP, keys), F32),
             pltpu.VMEM((rows * HP, keys), F32),
         ],
         compiler_params=pltpu.CompilerParams(
-            collective_id=0, has_side_effects=True, vmem_limit_bytes=50 * 1024 * 1024
+            collective_id=0, has_side_effects=True, vmem_limit_bytes=67043328
         ),
-    )(
-        single, angles, trans, left_factor, right_factor, chain, live, point_weight,
-        w_pair_in, chain_bias, w_pair_out, w_bias.T, out_gain, w_frame.T, w_query.T, w_qpoints.T,
-        w_keyval, w_kvpoints.T, w_out,
-    )
+    )(*args)
 
 
 def solution(mesh):

time: 45.4 us -> 38.6 us (0.85)
  local copies, waits for them, and re-layouts: 16 us -> 2.6 us
  Pallas kernels: 28.1 us -> 35 us
    unnamed x40 -> x2, local copies, waits for them, and re-layouts: 16 us -> 2.6 us
    pallas_call x1, Pallas kernels: 28.1 us -> 35 us  [per_device(): pl.pallas_call(functools.partial(kernel, n, (heads, head_dim, qpts, vpts,...]
where the time goes in v3:
time: 38.6 us; the launch traced here: 38.2 us
  Pallas kernels  35 us (91%)
  local copies, waits for them, and re-layouts  2.6 us (7%)
  between operations  0.65 us (2%)
    pallas_call x1, Pallas kernels, per_device(): pl.pallas_call(functools.partial(kernel, n, (heads, head_dim, qpts, vpts,...  35 us
    unnamed x2, local copies, waits for them, and re-layouts  2.6 us

profile of v3, /device:TPU:1, one launch (start us, length us, event | category | flops | bytes accessed | tf_op | source)
XLA Modules:
  0.0 38.2 jit_solution(13172414999269145864)
XLA Ops:
  0.6 35.0 %shard_map.194 = (bf16[16,384]{1,0:T(8,128)(2,1)}, f32[12,16]{1,0:T(8,128)}) custom-call(bf16[16,384]{1,0:T(8,128)(2,1)} %refs_0_.1, f32[3,16]{1,0:T(4,128)} %refs_1_.1, f32[3,16]{1,0:T(4,128)} %refs_2_.1, bf16[16,64]{1,0:T(8,128)(2,1)} %refs_3_.1, bf16[16,64]{1,0:T(8,128)(2,1)} %refs_4_.1, s32[16]{0:T(128)} %refs_5_.1, s32[16]{0:T(128)} %refs_6_.1, ...), custom_call_target="tpu_custom_call" | custom-call | tf_op jit(solution)/shard_map/pallas_call | solution.py:449
  35.6 1.3 %copy.23 = bf16[16,384]{1,0:T(8,128)(2,1)} copy(bf16[16,384]{1,0:T(8,128)(2,1)} %get-tuple-element.4) | data formatting | bytes 24576
  36.9 1.3 %copy.24 = f32[12,16]{1,0:T(8,128)} copy(f32[12,16]{1,0:T(8,128)} %get-tuple-element.5) | data formatting | bytes 1536
